TPU v7x, 32 devices: a whole 2x2x4 slice. The times are simulated.
32 devices in a mesh: row: 4 (over y, core), col: 8 (over z, x).
Axes of the slice: x: 2, y: 2, z: 4, core: 2. Of those that a mesh axis runs over, the one named last changes fastest.
Arguments:
- values: bfloat16 [8192, 128], P('row'), may hold values from -30 to 30
- points0: bfloat16 [2, 8192], P(None, 'row'), may hold values from 0 to 1
- points1: bfloat16 [2, 2048], P(None, 'row'), may hold values from 0 to 1
- points2: bfloat16 [2, 256], P(None, 'row'), may hold values from 0 to 1
- tiles_a0: int32 [4, 8, 2, 48], P('row', 'col'), may hold values from 0 to 15, as said below
- tiles_e1: int32 [4, 8, 2, 20], P('row', 'col'), may hold values from 0 to 15, as said below
- tiles_a1: int32 [4, 8, 2, 4], P('row', 'col'), may hold values from 0 to 3, as said below
- factor: bfloat16 [256, 256], P('row', 'col'), as said below
Outputs:
- fine_coef: float32 [8192, 128], P(('row', 'col'))
- mid_coef: float32 [2048, 128], P('col')
- coarse_coef: float32 [256, 128], P('row')
- norms: float32 [1], replicated
Inputs may be any that keep to these rules, and one draw needn't show every extreme that they name: `tiles_a0`: within each block the 48 listed tile pairs are distinct; tile rows are below 16 and tile columns below 8. `tiles_e1`: within each block the 20 listed tile pairs are distinct; tile rows are below 16 and tile columns below 2. `tiles_a1`: within each block the 4 listed tile pairs are distinct; tile rows are below 4 and tile columns below 2. `factor`: upper triangular; diagonal entries from 1 to 2.
All inputs are finite; a program needn't handle non-finite values.
Results may differ from a plain program's by a relative error of at most 0.0042.
Values may be sent and summed in bfloat16 or wider, within the bound.
A program may use at most 64 MiB of HBM per device.

v0:
```python
import math
import jax
import jax.numpy as jnp
from jax import lax
from jax.sharding import PartitionSpec as P

TILE = 128
support_fine = 0.35
support_mid = 0.55
support_coarse = 0.8


def spread(x, axis, root):
    mine = lax.axis_index(axis) == root
    return lax.psum(jnp.where(mine, x, jnp.zeros_like(x)), axis)


def wendland(left_pts, right_pts, support):
    left = left_pts.astype(jnp.float32)
    right = right_pts.astype(jnp.float32)
    across = left[0][..., :, None] - right[0][..., None, :]
    upward = left[1][..., :, None] - right[1][..., None, :]
    ratio_t = jnp.sqrt(across * across + upward * upward) / support
    margin = jnp.maximum(1.0 - ratio_t, 0.0)
    squared = margin * margin
    return (squared * squared * (4.0 * ratio_t + 1.0)).astype(jnp.bfloat16)


def listed_terms(row_pts, col_pts, listing, vector, support, flipped):
    row_tiles = row_pts.reshape(2, -1, TILE)
    col_tiles = col_pts.reshape(2, -1, TILE)
    listed = listing.shape[-1]
    group = math.gcd(listed, 32)
    order = listing.reshape(2, listed // group, group)
    fields = vector.shape[-1]
    inputs = vector.reshape(-1, TILE, fields)
    target = col_tiles.shape[1] if flipped else row_tiles.shape[1]
    total = jnp.zeros((target, TILE, fields), jnp.float32)

    def add_group(total, pair):
        tile_rows, tile_cols = pair
        kernel = wendland(row_tiles[:, tile_rows], col_tiles[:, tile_cols], support)
        if flipped:
            contrib = jnp.einsum(
                "gij,gir->gjr", kernel, inputs[tile_rows], preferred_element_type=jnp.float32
            )
            return (total.at[tile_cols].add(contrib), None)
        contrib = jnp.einsum(
            "gij,gjr->gir", kernel, inputs[tile_cols], preferred_element_type=jnp.float32
        )
        return (total.at[tile_rows].add(contrib), None)

    total, unused = lax.scan(add_group, total, (order[0], order[1]))
    return total.reshape(-1, fields)


def per_device(values, points0, points1, points2, tiles_a0, tiles_e1, tiles_a1, factor):
    row_count = lax.axis_size("row")
    col_count = lax.axis_size("col")
    col_id = lax.axis_index("col")
    col_per_row = col_count // row_count
    rows_fine, fields = values.shape
    rows_mid = points1.shape[1]
    share = rows_fine // col_count
    cols_fine = rows_fine // col_per_row
    cols_mid = rows_mid // col_per_row
    source = col_id // col_per_row
    part_index = col_id % col_per_row
    value_piece = lax.dynamic_slice_in_dim(values, part_index * cols_fine, cols_fine, 0)
    fine_piece = lax.dynamic_slice_in_dim(points0, part_index * cols_fine, cols_fine, 1)
    mid_piece = lax.dynamic_slice_in_dim(points1, part_index * cols_mid, cols_mid, 1)
    value_cols, fine_cols, mid_cols = (
        spread(value_piece, "row", source),
        spread(fine_piece, "row", source),
        spread(mid_piece, "row", source),
    )
    scale_a0 = (rows_fine / (col_count * tiles_a0.shape[-1] * TILE * TILE)) ** 0.5
    scale_e1 = (rows_fine / (col_count * tiles_e1.shape[-1] * TILE * TILE)) ** 0.5
    scale_a1 = (rows_mid / (col_count * tiles_a1.shape[-1] * TILE * TILE)) ** 0.5
    scale_e2 = (1.0 / (rows_mid * row_count)) ** 0.5
    fine_data = values.astype(jnp.float32)
    own_data = lax.dynamic_slice_in_dim(values, col_id * share, share, 0).astype(jnp.float32)
    product_part = listed_terms(points0, fine_cols, tiles_a0[0, 0], value_cols, support_fine, False)
    product_whole = lax.psum(product_part, "col")
    fine_residual = fine_data - 0.5 * (scale_a0 * product_whole)
    fine_square = jnp.sum(fine_residual * fine_residual)
    restrict_part = listed_terms(
        points0, mid_cols, tiles_e1[0, 0], fine_residual.astype(jnp.bfloat16), support_mid, True
    )
    restrict_sum = lax.psum(restrict_part, "row")
    mid_data = scale_e1 * restrict_sum
    mid_part = listed_terms(
        points1, mid_cols, tiles_a1[0, 0], mid_data.astype(jnp.bfloat16), support_mid, False
    )
    mid_whole = (scale_a1 * lax.psum(mid_part, "col")).astype(jnp.bfloat16)
    mid_slice = lax.dynamic_slice_in_dim(mid_whole, part_index * cols_mid, cols_mid, 0)
    mid_turned = spread(mid_slice, "row", source)
    mid_residual = mid_data - 0.5 * mid_turned.astype(jnp.float32)
    coarse_kernel = wendland(points2, mid_cols, support_coarse)
    coarse_part = jnp.dot(
        coarse_kernel, mid_residual.astype(jnp.bfloat16), preferred_element_type=jnp.float32
    )
    coarse_sum = lax.psum(coarse_part, "col")
    coarse_data = (scale_e2 * coarse_sum).astype(jnp.bfloat16)
    halfway_part = lax.dot_general(
        factor, coarse_data, (((0,), (0,)), ((), ())), preferred_element_type=jnp.float32
    )
    halfway = lax.psum(halfway_part, "row").astype(jnp.bfloat16)
    coarse_part_two = jnp.dot(factor, halfway, preferred_element_type=jnp.float32)
    coarse_coef = lax.psum(coarse_part_two, "col")
    prolong_part = lax.dot_general(
        coarse_kernel,
        coarse_coef.astype(jnp.bfloat16),
        (((0,), (0,)), ((), ())),
        preferred_element_type=jnp.float32,
    )
    mid_coef = 0.5 * mid_data + scale_e2 * lax.psum(prolong_part, "row")
    fine_part = listed_terms(
        points0, mid_cols, tiles_e1[0, 0], mid_coef.astype(jnp.bfloat16), support_mid, False
    )
    fine_coef = 0.5 * own_data + scale_e1 * lax.psum_scatter(
        fine_part, "col", scatter_dimension=0, tiled=True
    )
    fine_total = lax.psum(fine_square / col_count, ("row", "col"))
    fine_norm = fine_total / (rows_fine * row_count * fields)
    return (fine_coef, mid_coef, coarse_coef, jnp.stack([fine_norm]))


def solution(mesh):
    return jax.shard_map(
        per_device,
        mesh=mesh,
        in_specs=(
            P("row", None),
            P(None, "row"),
            P(None, "row"),
            P(None, "row"),
            P("row", "col", None, None),
            P("row", "col", None, None),
            P("row", "col", None, None),
            P("row", "col"),
        ),
        out_specs=(P(("row", "col"), None), P("col", None), P("row", None), P()),
        check_vma=False,
    )
```

profile of v0, /device:TPU:0, one launch (start us, length us, event | category | flops | bytes accessed | tf_op | source)
XLA Modules:
  0.0 501.4 jit_solution(3732552858694689181)
XLA Ops:
  7.3 1.7 dynamic-slice_select_fusion
  11.9 8.5 %all-reduce = (bf16[2,256]{1,0:T(2,128)(2,1)S(1)}, bf16[2,8,128]{2,0,1:T(2,128)(2,1)S(1)}) all-reduce(bf16[2,256]{1,0:T(2,128)(2,1)S(1)} %broadcast_select_fusion.1, bf16[2,8,128]{2,0,1:T(2,128)(2,1)S(1)} %fusion.64), channel_id=1, replica_groups=mesh['row'=4,'col'=8] {'row'}, use_global_device_ids=true, to_apply=%region_0.1 | all-reduce | flops 2560 | bytes 10240 | tf_op jit(solution)/shard_map/psum | solution.py:15
  20.4 24.9 %all-reduce.8.cloned.1.call-done = bf16[8,128,128]{2,1,0:T(8,128)(2,1)} async-done(((bf16[8,128,128]{2,1,0:T(8,128)(2,1)}), bf16[8,128,128]{2,1,0:T(8,128)(2,1)}) %all-reduce.8.cloned.1.call-update) | async-done | bytes 262160 | tf_op jit(solution)/shard_map/psum | solution.py:15
  46.3 15.2 %while.40 = (s32[]{:T(128)}, f32[16,128,128]{2,1,0:T(8,128)S(1)}, s32[3,16]{1,0:T(4,128)S(1)}, bf16[2,16,128]{2,0,1:T(2,128)(2,1)S(1)}, s32[3,16]{1,0:T(4,128)S(...) while((s32[]{:T(128)}, f32[16,128,128]{2,1,0:T(8,128)S(1)}, ...), condition=%wide.region_5.6_spmd, body=%wide.region_3.5_spmd.sunk | while | flops 71051360 | bytes 5956313 | solution.py:53
  48.2 1.5 fusion.118
  49.7 1.6 scatter_fusion
  54.8 1.6 scatter_fusion
  59.9 1.6 scatter_fusion
  63.9 77.0 %all-reduce.10.cloned.1.call-done = f32[2048,128]{1,0:T(8,128)} async-done(((f32[2048,128]{1,0:T(8,128)}), f32[2048,128]{1,0:T(8,128)}) %all-reduce.10.cloned.1.call-update) | async-done | bytes 1048592 | tf_op jit(solution)/shard_map/psum | solution.py:84
  140.9 2.2 multiply_reduce_fusion
  143.1 14.7 %while.41 = (s32[]{:T(128)}, f32[2,128,128]{2,1,0:T(8,128)S(1)}, s32[5,4]{1,0:T(8,128)S(1)}, s32[5,4]{1,0:T(8,128)S(1)}, bf16[2,16,128]{2,0,1:T(2,128)(2,1)S(1)}...) while((s32[]{:T(128)}, f32[2,128,128]{2,1,0:T(8,128)S(1)}, ...), condition=%wide.region_9.10_spmd, body=%wide.region_7.9_spmd.sunk | while | flops 17764376 | bytes 1495289 | solution.py:53
  158.6 31.5 %all-reduce.12.cloned.1.call-done = f32[256,128]{1,0:T(8,128)} async-done(((f32[256,128]{1,0:T(8,128)}), f32[256,128]{1,0:T(8,128)}) %all-reduce.12.cloned.1.call-update) | async-done | bytes 131088 | tf_op jit(solution)/shard_map/psum | solution.py:90
  193.5 71.1 %all-reduce.14.cloned.1.call-done = f32[512,128]{1,0:T(8,128)} async-done(((f32[512,128]{1,0:T(8,128)}), f32[512,128]{1,0:T(8,128)}) %all-reduce.14.cloned.1.call-update) | async-done | bytes 262160 | tf_op jit(solution)/shard_map/psum | solution.py:95
  264.6 1.6 fusion.57
  266.2 31.9 %all-reduce.16.cloned.1.call-done = bf16[256,128]{1,0:T(8,128)(2,1)} async-done(((bf16[256,128]{1,0:T(8,128)(2,1)}), bf16[256,128]{1,0:T(8,128)(2,1)}) %all-reduce.16.cloned.1.call-update) | async-done | bytes 65552 | tf_op jit(solution)/shard_map/psum | solution.py:15
  299.2 37.1 %psum.91 = f32[64,128]{1,0:T(8,128)S(1)} all-reduce(f32[64,128]{1,0:T(8,128)S(1)} %fusion.56), channel_id=1, replica_groups=mesh['row'=4,'col'=8] {'col'}, use_global_device_ids=true, to_apply=%region_14.15 | all-reduce | flops 8192 | bytes 65536 | tf_op jit(solution)/shard_map/psum | solution.py:103
  336.5 10.8 %psum.92 = bf16[32,128]{0,1:T(8,128)(2,1)S(1)} all-reduce(f32[32,128]{0,1:T(8,128)S(1)} %convolution_bitcast_fusion), channel_id=1, replica_groups=mesh['row'=4,'col'=8] {'row'}, use_global_device_ids=true, to_apply=%region_15.16 | all-reduce | flops 4096 | bytes 24576 | tf_op jit(solution)/shard_map/psum | solution.py:108
  347.5 33.0 %psum.93 = f32[64,128]{1,0:T(8,128)S(1)} all-reduce(f32[64,128]{1,0:T(8,128)S(1)} %convolution_bitcast_fusion.1), channel_id=1, replica_groups=mesh['row'=4,'col'=8] {'col'}, use_global_device_ids=true, to_apply=%region_16.17 | all-reduce | flops 8192 | bytes 65536 | tf_op jit(solution)/shard_map/psum | solution.py:110
  381.6 28.0 %all-reduce.18.cloned.1.call-done = f32[256,128]{1,0:T(8,128)} async-done(((f32[256,128]{1,0:T(8,128)}), f32[256,128]{1,0:T(8,128)}) %all-reduce.18.cloned.1.call-update) | async-done | bytes 131088 | tf_op jit(solution)/shard_map/psum | solution.py:117
  409.5 1.6 fusion.82
  411.2 14.8 %while.42 = (s32[]{:T(128)}, f32[16,128,128]{2,1,0:T(8,128)S(1)}, s32[5,4]{1,0:T(8,128)S(1)}, bf16[2,16,128]{2,0,1:T(2,128)(2,1)S(1)}, s32[5,4]{1,0:T(8,128)S(1)...) while((s32[]{:T(128)}, f32[16,128,128]{2,1,0:T(8,128)S(1)}, ...), condition=%wide.region_20.21_spmd, body=%wide.region_18.20_spmd.sunk | while | flops 17764376 | bytes 1495289 | solution.py:53
  427.7 39.5 %psum.95 = f32[]{:T(128)} all-reduce(f32[]{:T(128)S(6)} %div.39), channel_id=1, replica_groups=mesh['row'=4,'col'=8] {'row','col'}, use_global_device_ids=true, to_apply=%region_23.24 | all-reduce | flops 1 | bytes 8 | tf_op jit(solution)/shard_map/psum | solution.py:124
  467.8 24.0 %reduce-scatter.2.cloned.1.call-done = f32[256,128]{1,0:T(8,128)} async-done(((f32[2048,128]{1,0:T(8,128)}), f32[256,128]{1,0:T(8,128)}) %reduce-scatter.2.cloned.1.call-update) | async-done | bytes 131088 | tf_op jit(solution)/shard_map/reduce_scatter | solution.py:121
  491.8 1.6 multiply_add_fusion
  (228 shorter events, 51.4 us)
Async XLA Ops:
  7.2 329.1 %copy-start = (bf16[64,32]{0,1:T(8,128)(2,1)S(1)}, bf16[64,32]{0,1:T(8,128)(2,1)}, u32[]{:S(2)}) copy-start(bf16[64,32]{0,1:T(8,128)(2,1)} %param.21) | copy-start | bytes 12292
  7.2 38.2 %all-reduce.8.cloned.1.call-start = ((), (), s32[]{:S(2)}) async-start(), calls=%async_computation.1 | async-start | bytes 524288 | tf_op jit(solution)/shard_map/psum | solution.py:15
  9.0 131.9 %all-reduce.10.cloned.1.call-start = ((), (), s32[]{:S(2)}) async-start(), calls=%async_computation.2 | async-start | bytes 2097152 | tf_op jit(solution)/shard_map/psum | solution.py:84
  9.0 0.7 copy-start.11
  9.7 0.7 copy-start.12
  10.4 0.7 copy-start.10
  11.2 0.7 copy-start.8
  45.4 0.9 copy-start.2
  61.5 1.0 copy-start.1
  61.5 1.1 copy-start.13
  61.6 79.4 %copy-start.6 = (bf16[2048,128]{1,0:T(8,128)(2,1)S(1)}, bf16[2048,128]{1,0:T(8,128)(2,1)}, u32[]{:S(2)}) copy-start(bf16[2048,128]{1,0:T(8,128)(2,1)} %param.14) | copy-start | bytes 1572868
  62.6 127.5 %all-reduce.12.cloned.1.call-start = ((), (), s32[]{:S(2)}) async-start(), calls=%async_computation.3 | async-start | bytes 262144 | tf_op jit(solution)/shard_map/psum | solution.py:90
  157.9 0.7 copy-start.3
  158.5 106.1 %all-reduce.14.cloned.1.call-start = ((), (), s32[]{:S(2)}) async-start(), calls=%async_computation.4 | async-start | bytes 524288 | tf_op jit(solution)/shard_map/psum | solution.py:95
  192.7 0.7 copy-start.5
  192.7 0.8 copy-start.14
  193.4 104.7 %all-reduce.16.cloned.1.call-start = ((), (), s32[]{:S(2)}) async-start(), calls=%async_computation.5 | async-start | bytes 131072 | tf_op jit(solution)/shard_map/psum | solution.py:15
  193.5 104.6 %copy-start.7 = (f32[256,128]{1,0:T(8,128)S(1)}, f32[256,128]{1,0:T(8,128)}, u32[]{:S(2)}) copy-start(f32[256,128]{1,0:T(8,128)} %all-reduce.12.cloned.1.call-done) | copy-start | bytes 393220
  266.2 143.4 %all-reduce.18.cloned.1.call-start = ((), (), s32[]{:S(2)}) async-start(), calls=%async_computation.6 | async-start | bytes 262144 | tf_op jit(solution)/shard_map/psum | solution.py:117
  380.5 1.0 copy-start.9
  381.5 110.3 %reduce-scatter.2.cloned.1.call-start = ((), (), s32[]{:S(2)}) async-start(), calls=%async_computation.7 | async-start | bytes 1179648 | tf_op jit(solution)/shard_map/reduce_scatter | solution.py:121
  426.0 1.0 copy-start.4
Sparse Core Ops, SparseCore 0:
  10.3 34.9 all-reduce.7
  62.7 78.1 all-reduce.9
  158.7 31.3 all-reduce.11
  193.6 70.9 all-reduce.13
  267.3 30.7 all-reduce.15
  381.6 27.8 all-reduce.17
  427.2 64.5 reduce-scatter.1
where the time goes:
time: 502 us; the launch traced here: 501 us
  waiting for transfers between devices  288 us (57%)
  blocking collectives  129 us (26%)
  local copies, waits for them, and re-layouts  31.9 us (6%)
  other arithmetic  23.1 us (5%)
  between operations  16.8 us (3%)
  matrix products  10.9 us (2%)
    psum x1, waiting for transfers between devices, per_device(): product_whole = lax.psum(product_part, 'col')  77 us
    psum x1, waiting for transfers between devices, per_device(): mid_whole = (scale_a1 * lax.psum(mid_part, 'col')).astype(jnp.bfloat16)  71.1 us
    psum x2, waiting for transfers between devices, spread(): return lax.psum(jnp.where(mine, x, jnp.zeros_like(x)), axis)  56.8 us
    psum x1, blocking collectives, per_device(): fine_total = lax.psum(fine_square / col_count, ('row', 'col'))  39.5 us
    psum x1, blocking collectives, per_device(): coarse_sum = lax.psum(coarse_part, 'col')  37.1 us
    psum x1, blocking collectives, per_device(): coarse_coef = lax.psum(coarse_part_two, 'col')  33 us
    psum x1, waiting for transfers between devices, per_device(): restrict_sum = lax.psum(restrict_part, 'row')  31.5 us
    psum x1, waiting for transfers between devices, per_device(): mid_coef = 0.5 * mid_data + scale_e2 * lax.psum(prolong_part, 'row')  28 us
  transfers between devices with their start and end apart: 7, of which 7 were waited for; matrix products, arithmetic and copies ran while one was open for 0% of the time, Pallas kernels for 0%

commit v1 on v0

--- a/solution.py
+++ b/solution.py
@@ -87,7 +87,7 @@
     restrict_part = listed_terms(
         points0, mid_cols, tiles_e1[0, 0], fine_residual.astype(jnp.bfloat16), support_mid, True
     )
-    restrict_sum = lax.psum(restrict_part, "row")
+    restrict_sum = jnp.sum(lax.all_gather(restrict_part, "row"), axis=0)
     mid_data = scale_e1 * restrict_sum
     mid_part = listed_terms(
         points1, mid_cols, tiles_a1[0, 0], mid_data.astype(jnp.bfloat16), support_mid, False

time: 502 us -> 474 us (0.944)
  waiting for transfers between devices: 288 us -> 256 us
  blocking collectives: 129 us -> 136 us
    psum x1 -> x0, waiting for transfers between devices: 31.5 us -> none  [per_device(): restrict_sum = lax.psum(restrict_part, 'row')]
    all_gather x0 -> x1, blocking collectives: none -> 7.15 us  [per_device(): restrict_sum = jnp.sum(lax.all_gather(restrict_part, 'row'), axis=0)]
  transfers between devices with their start and end apart: 7 -> 6, of which waited for: 7 -> 6; matrix products, arithmetic and copies ran while one was open for 0% -> 0% of each run, Pallas kernels for 0% -> 0%
where the time goes in v1:
time: 474 us
  waiting for transfers between devices  256 us (54%)
  blocking collectives  136 us (29%)
  local copies, waits for them, and re-layouts  31.4 us (7%)
  other arithmetic  22.2 us (5%)
  between operations  16.8 us (4%)
  matrix products  10.9 us (2%)
    psum x1, waiting for transfers between devices, per_device(): product_whole = lax.psum(product_part, 'col')  76.9 us
    psum x1, waiting for transfers between devices, per_device(): mid_whole = (scale_a1 * lax.psum(mid_part, 'col')).astype(jnp.bfloat16)  70 us
    psum x2, waiting for transfers between devices, spread(): return lax.psum(jnp.where(mine, x, jnp.zeros_like(x)), axis)  56.6 us
    psum x1, blocking collectives, per_device(): fine_total = lax.psum(fine_square / col_count, ('row', 'col'))  39.6 us
    psum x1, blocking collectives, per_device(): coarse_sum = lax.psum(coarse_part, 'col')  37.1 us
    psum x1, blocking collectives, per_device(): coarse_coef = lax.psum(coarse_part_two, 'col')  33 us
    psum x1, waiting for transfers between devices, per_device(): mid_coef = 0.5 * mid_data + scale_e2 * lax.psum(prolong_part, 'row')  28.1 us
    reduce_scatter x1, waiting for transfers between devices, per_device(): lax.psum_scatter(fine_part, 'col', scatter_dimension=0, tiled=True)  23.9 us
  transfers between devices with their start and end apart: 6, of which 6 were waited for; matrix products, arithmetic and copies ran while one was open for 0% of the time, Pallas kernels for 0%

profile of v1, /device:TPU:0, one launch (start us, length us, event | category | flops | bytes accessed | tf_op | source)
XLA Modules:
  0.0 473.8 jit_solution(5491270841488756216)
XLA Ops:
  7.3 1.7 dynamic-slice_select_fusion
  11.9 8.7 %all-reduce = (bf16[2,256]{1,0:T(2,128)(2,1)S(1)}, bf16[2,8,128]{2,0,1:T(2,128)(2,1)S(1)}) all-reduce(bf16[2,256]{1,0:T(2,128)(2,1)S(1)} %broadcast_select_fusion.1, bf16[2,8,128]{2,0,1:T(2,128)(2,1)S(1)} %fusion.64), channel_id=1, replica_groups=mesh['row'=4,'col'=8] {'row'}, use_global_device_ids=true, to_apply=%region_0.1 | all-reduce | flops 2560 | bytes 10240 | tf_op jit(solution)/shard_map/psum | solution.py:15
  20.7 24.7 %all-reduce.7.cloned.1.call-done = bf16[8,128,128]{2,1,0:T(8,128)(2,1)} async-done(((bf16[8,128,128]{2,1,0:T(8,128)(2,1)}), bf16[8,128,128]{2,1,0:T(8,128)(2,1)}) %all-reduce.7.cloned.1.call-update) | async-done | bytes 262160 | tf_op jit(solution)/shard_map/psum | solution.py:15
  46.3 15.2 %while.40 = (s32[]{:T(128)}, f32[16,128,128]{2,1,0:T(8,128)S(1)}, s32[3,16]{1,0:T(4,128)S(1)}, bf16[2,16,128]{2,0,1:T(2,128)(2,1)S(1)}, s32[3,16]{1,0:T(4,128)S(...) while((s32[]{:T(128)}, f32[16,128,128]{2,1,0:T(8,128)S(1)}, ...), condition=%wide.region_5.6_spmd, body=%wide.region_3.5_spmd.sunk | while | flops 71051360 | bytes 5956313 | solution.py:53
  48.2 1.5 fusion.118
  49.7 1.6 scatter_fusion
  54.8 1.6 scatter_fusion
  59.9 1.6 scatter_fusion
  64.0 76.9 %all-reduce.9.cloned.1.call-done = f32[2048,128]{1,0:T(8,128)} async-done(((f32[2048,128]{1,0:T(8,128)}), f32[2048,128]{1,0:T(8,128)}) %all-reduce.9.cloned.1.call-update) | async-done | bytes 1048592 | tf_op jit(solution)/shard_map/psum | solution.py:84
  140.9 2.2 multiply_reduce_fusion
  143.1 14.8 %while.41 = (s32[]{:T(128)}, f32[2,128,128]{2,1,0:T(8,128)S(1)}, s32[5,4]{1,0:T(8,128)S(1)}, s32[5,4]{1,0:T(8,128)S(1)}, bf16[2,16,128]{2,0,1:T(2,128)(2,1)S(1)}...) while((s32[]{:T(128)}, f32[2,128,128]{2,1,0:T(8,128)S(1)}, ...), condition=%wide.region_9.10_spmd, body=%wide.region_7.9_spmd.sunk | while | flops 17764376 | bytes 1495289 | solution.py:53
  157.9 7.2 %all_gather.3 = f32[4,256,128]{2,1,0:T(8,128)S(1)} all-gather(f32[1,256,128]{2,1,0:T(8,128)S(1)} %bitcast.150), channel_id=1, replica_groups=mesh['row'=4,'col'=8] {'row'}, dimensions={0}, use_global_device_ids=true | all-gather | bytes 655360 | tf_op jit(solution)/shard_map/all_gather | solution.py:90
  167.6 70.0 %all-reduce.11.cloned.1.call-done = f32[512,128]{1,0:T(8,128)} async-done(((f32[512,128]{1,0:T(8,128)}), f32[512,128]{1,0:T(8,128)}) %all-reduce.11.cloned.1.call-update) | async-done | bytes 262160 | tf_op jit(solution)/shard_map/psum | solution.py:95
  237.6 1.6 fusion.57
  239.3 31.9 %all-reduce.13.cloned.1.call-done = bf16[256,128]{1,0:T(8,128)(2,1)} async-done(((bf16[256,128]{1,0:T(8,128)(2,1)}), bf16[256,128]{1,0:T(8,128)(2,1)}) %all-reduce.13.cloned.1.call-update) | async-done | bytes 65552 | tf_op jit(solution)/shard_map/psum | solution.py:15
  272.2 37.1 %psum.83 = f32[64,128]{1,0:T(8,128)S(1)} all-reduce(f32[64,128]{1,0:T(8,128)S(1)} %fusion.56), channel_id=1, replica_groups=mesh['row'=4,'col'=8] {'col'}, use_global_device_ids=true, to_apply=%region_14.15 | all-reduce | flops 8192 | bytes 65536 | tf_op jit(solution)/shard_map/psum | solution.py:103
  309.4 10.2 %psum.84 = bf16[32,128]{1,0:T(8,128)(2,1)S(1)} all-reduce(f32[32,128]{1,0:T(8,128)S(1)} %convolution_bitcast_fusion.1), channel_id=1, replica_groups=mesh['row'=4,'col'=8] {'row'}, use_global_device_ids=true, to_apply=%region_15.16 | all-reduce | flops 4096 | bytes 24576 | tf_op jit(solution)/shard_map/psum | solution.py:108
  319.8 33.0 %psum.85 = f32[64,128]{1,0:T(8,128)S(1)} all-reduce(f32[64,128]{1,0:T(8,128)S(1)} %convolution_bitcast_fusion), channel_id=1, replica_groups=mesh['row'=4,'col'=8] {'col'}, use_global_device_ids=true, to_apply=%region_16.17 | all-reduce | flops 8192 | bytes 65536 | tf_op jit(solution)/shard_map/psum | solution.py:110
  353.9 28.1 %all-reduce.15.cloned.1.call-done = f32[256,128]{1,0:T(8,128)} async-done(((f32[256,128]{1,0:T(8,128)}), f32[256,128]{1,0:T(8,128)}) %all-reduce.15.cloned.1.call-update) | async-done | bytes 131088 | tf_op jit(solution)/shard_map/psum | solution.py:117
  382.0 1.6 fusion.82
  383.6 14.8 %while.42 = (s32[]{:T(128)}, f32[16,128,128]{2,1,0:T(8,128)S(1)}, s32[5,4]{1,0:T(8,128)S(1)}, bf16[2,16,128]{2,0,1:T(2,128)(2,1)S(1)}, s32[5,4]{1,0:T(8,128)S(1)...) while((s32[]{:T(128)}, f32[16,128,128]{2,1,0:T(8,128)S(1)}, ...), condition=%wide.region_20.21_spmd, body=%wide.region_18.20_spmd.sunk | while | flops 17764376 | bytes 1495289 | solution.py:53
  400.1 39.6 %psum.87 = f32[]{:T(128)} all-reduce(f32[]{:T(128)S(6)} %div.39), channel_id=1, replica_groups=mesh['row'=4,'col'=8] {'row','col'}, use_global_device_ids=true, to_apply=%region_23.24 | all-reduce | flops 1 | bytes 8 | tf_op jit(solution)/shard_map/psum | solution.py:124
  440.3 23.9 %reduce-scatter.2.cloned.1.call-done = f32[256,128]{1,0:T(8,128)} async-done(((f32[2048,128]{1,0:T(8,128)}), f32[256,128]{1,0:T(8,128)}) %reduce-scatter.2.cloned.1.call-update) | async-done | bytes 131088 | tf_op jit(solution)/shard_map/reduce_scatter | solution.py:121
  464.2 1.6 multiply_add_fusion
  (223 shorter events, 50.0 us)
Async XLA Ops:
  7.2 302.1 %copy-start = (bf16[64,32]{0,1:T(8,128)(2,1)S(1)}, bf16[64,32]{0,1:T(8,128)(2,1)}, u32[]{:S(2)}) copy-start(bf16[64,32]{0,1:T(8,128)(2,1)} %param.21) | copy-start | bytes 12292
  7.2 38.2 %all-reduce.7.cloned.1.call-start = ((), (), s32[]{:S(2)}) async-start(), calls=%async_computation.1 | async-start | bytes 524288 | tf_op jit(solution)/shard_map/psum | solution.py:15
  9.0 0.7 copy-start.6
  9.0 131.9 %all-reduce.9.cloned.1.call-start = ((), (), s32[]{:S(2)}) async-start(), calls=%async_computation.2 | async-start | bytes 2097152 | tf_op jit(solution)/shard_map/psum | solution.py:84
  9.7 0.7 copy-start.9
  10.4 0.7 copy-start.10
  11.0 0.7 copy-start.8
  11.9 8.7 %copy-start.11 = (s32[1,1,2,20]{3,2,1,0:T(2,128)S(1)}, s32[1,1,2,20]{3,2,1,0:T(2,128)}, u32[]{:S(2)}) copy-start(s32[1,1,2,20]{3,2,1,0:T(2,128)} %param.19) | copy-start | bytes 484
  45.4 0.9 copy-start.2
  61.5 1.0 copy-start.1
  61.5 79.4 %copy-start.5 = (bf16[2048,128]{1,0:T(8,128)(2,1)S(1)}, bf16[2048,128]{1,0:T(8,128)(2,1)}, u32[]{:S(2)}) copy-start(bf16[2048,128]{1,0:T(8,128)(2,1)} %param.14) | copy-start | bytes 1572868
  62.6 175.0 %all-reduce.11.cloned.1.call-start = ((), (), s32[]{:S(2)}) async-start(), calls=%async_computation.3 | async-start | bytes 524288 | tf_op jit(solution)/shard_map/psum | solution.py:95
  166.8 0.7 copy-start.4
  166.8 0.8 copy-start.12
  167.5 103.6 %all-reduce.13.cloned.1.call-start = ((), (), s32[]{:S(2)}) async-start(), calls=%async_computation.4 | async-start | bytes 131072 | tf_op jit(solution)/shard_map/psum | solution.py:15
  239.2 142.8 %all-reduce.15.cloned.1.call-start = ((), (), s32[]{:S(2)}) async-start(), calls=%async_computation.5 | async-start | bytes 262144 | tf_op jit(solution)/shard_map/psum | solution.py:117
  352.8 1.0 copy-start.7
  353.8 110.4 %reduce-scatter.2.cloned.1.call-start = ((), (), s32[]{:S(2)}) async-start(), calls=%async_computation.6 | async-start | bytes 1179648 | tf_op jit(solution)/shard_map/reduce_scatter | solution.py:121
  398.4 1.0 copy-start.3
Sparse Core Ops, SparseCore 0:
  10.3 34.9 all-reduce.6
  62.7 78.1 all-reduce.8
  167.6 69.9 all-reduce.10
  240.4 30.7 all-reduce.12
  353.9 27.9 all-reduce.14
  399.6 64.5 reduce-scatter.1
